TPU v7x, 256 devices: a whole 4x4x8 slice. The times are simulated.
256 devices in a mesh: mp: 32 (over x, z), dp: 8 (over y, core).
Axes of the slice: x: 4, y: 4, z: 8, core: 2. Of those that a mesh axis runs over, the one named last changes fastest.
Arguments:
- tables: bfloat16 [20, 65536, 128], P(None, 'mp'), may hold values from -3 to 3
- block_rows: int32 [16384, 128], P(('mp', 'dp')), may hold values from 0 to 2047
- block_slots: int32 [16384, 128], P(('mp', 'dp')), may hold values from 0 to 127
- block_table: int32 [16384], P(('mp', 'dp')), may hold values from 0 to 19
- block_peer: int32 [16384, 1], P(('mp', 'dp')), may hold values from 0 to 31; in each aligned block of 64 rows (0 to 63, 64 to 127, ...) at most 4 rows name the same one
- block_len: int32 [16384], P(('mp', 'dp')), may hold values from 1 to 128
- block_count: int32 [256], P(('mp', 'dp')), may hold values from 1 to 64, as said below
- cross_in: bfloat16 [4, 2560, 256], P(None, 'dp'), may hold values from -0.23632812 to 0.23632812
- cross_mix: bfloat16 [4, 256, 256], replicated, may hold values from -0.5625 to 0.5625
- cross_out: bfloat16 [4, 256, 2560], P(None, None, 'dp'), may hold values from -0.375 to 0.375
- cross_bias: float32 [4, 2560], replicated, may hold values from -3 to 3
- gate_weight: bfloat16 [4, 2560], replicated, may hold values from -0.47265625 to 0.47265625
Outputs:
- crossed: bfloat16 [32768, 2560], P(('mp', 'dp'))
Inputs may be any that keep to these rules, and one draw needn't show every extreme that they name: `block_peer`: in the 64 blocks of one device no destination is named by more than 4 blocks, a bound that the blocks of some device reach. The live blocks of a device are its first block_count blocks; some device has exactly 64. Entries of a block at positions below its block_len are live. `block_rows`: A row index within the device's own shard of the table. `block_slots`: A sample of the destination device.
All inputs are finite; a program needn't handle non-finite values.
Results may differ from a plain program's by a relative error of at most 0.0059.
Values may be sent and summed in bfloat16 or wider, within the bound.
No kernel may reach another device: no remote copies, remote signals or barrier semaphores. Data moves between devices by JAX's collectives and lax.ppermute only.
A program may use at most 128 MiB of HBM per device.

v0:
```python
import jax
import jax.numpy as jnp
from jax import lax
from jax.sharding import PartitionSpec as P

B_DEV = 128


blocks_per_turn = 8


def pick_rows(tables, block_rows, block_table, first):
    row_ids = lax.dynamic_slice_in_dim(block_rows, first, blocks_per_turn, 0)
    table_ids = lax.dynamic_slice_in_dim(block_table, first, blocks_per_turn, 0)
    return tables[table_ids[:, None], row_ids]


def on_device(
    tables,
    block_rows,
    block_slots,
    block_table,
    block_peer,
    block_len,
    block_count,
    cross_in,
    cross_mix,
    cross_out,
    cross_bias,
    gate_weight,
):
    peers = lax.axis_size("mp")
    total_blocks, block_width = block_rows.shape
    table_count, rows_dev, width = tables.shape
    samples = B_DEV
    count = block_count[0]
    turns = (count + blocks_per_turn - 1) // blocks_per_turn
    peer_ids = block_peer[:, 0]
    entries = jnp.arange(block_width, dtype=jnp.int32)
    sample_ids = jnp.arange(samples, dtype=jnp.int32)
    capacity = max(2, 2 * total_blocks // peers)

    def gather_turn(turn, store):
        first = turn * blocks_per_turn
        picked = pick_rows(tables, block_rows, block_table, first)
        return lax.dynamic_update_slice_in_dim(store, picked, first, 0)

    stored = lax.fori_loop(
        0, turns, gather_turn, jnp.zeros((total_blocks, block_width, width), jnp.bfloat16)
    )
    live_block = jnp.arange(total_blocks, dtype=jnp.int32) < count
    peer_table = (
        (peer_ids[:, None] == jnp.arange(peers, dtype=jnp.int32)[None, :]) & live_block[:, None]
    ).astype(jnp.int32)
    before = jnp.cumsum(peer_table, axis=0) - peer_table
    position = jnp.sum(before * peer_table, axis=1)
    target = jnp.where(live_block, peer_ids * capacity + position, peers * capacity)
    live_entry = (entries[None, :] < block_len[:, None]) & live_block[:, None]
    code = jnp.where(live_entry, block_table[:, None] * samples + block_slots, -1)
    send_rows = (
        jnp.zeros((peers * capacity, block_width, width), jnp.bfloat16)
        .at[target]
        .set(stored, mode="drop")
    )
    send_code = (
        jnp.full((peers * capacity, block_width), -1, jnp.int32).at[target].set(code, mode="drop")
    )
    arrived_rows, arrived_code = (
        lax.all_to_all(
            send_rows.reshape(peers, capacity, block_width, width),
            "mp",
            split_axis=0,
            concat_axis=0,
            tiled=True,
        ),
        lax.all_to_all(
            send_code.reshape(peers, capacity, block_width),
            "mp",
            split_axis=0,
            concat_axis=0,
            tiled=True,
        ),
    )
    flat_rows = arrived_rows.reshape(peers * capacity, block_width, width)
    flat_code = arrived_code.reshape(peers * capacity, block_width)
    slot_of = jnp.where(flat_code >= 0, flat_code % samples, -1)
    onehot = (slot_of[:, :, None] == sample_ids[None, None, :]).astype(jnp.bfloat16)
    contrib = jnp.einsum("kis,kiw->ksw", onehot, flat_rows, preferred_element_type=jnp.float32)
    top_code = jnp.max(flat_code, axis=1)
    slot_live = top_code >= 0
    table_of = jnp.maximum(top_code, 0) // samples
    table_grid = table_of.reshape(peers, capacity)
    live_grid = slot_live.reshape(peers, capacity)
    same = (
        (table_grid[:, :, None] == table_grid[:, None, :])
        & live_grid[:, :, None]
        & live_grid[:, None, :]
    )
    grouped = jnp.einsum(
        "pkj,pjx->pkx", same.astype(jnp.float32), contrib.reshape(peers, capacity, samples * width)
    )
    rounded = grouped.astype(jnp.bfloat16).astype(jnp.float32)
    slot_order = jnp.arange(capacity, dtype=jnp.int32)
    earlier = jnp.sum(same & (slot_order[None, None, :] < slot_order[None, :, None]), axis=2)
    leader = (live_grid & (earlier == 0)).reshape(peers * capacity)
    owner = (
        (table_of[:, None] == jnp.arange(table_count, dtype=jnp.int32)[None, :]) & leader[:, None]
    ).astype(jnp.float32)
    summed = jnp.einsum("kt,kx->tx", owner, rounded.reshape(peers * capacity, samples * width))
    embedded = (
        summed.reshape(table_count, samples, width)
        .transpose(1, 0, 2)
        .reshape(samples, table_count * width)
        .astype(jnp.bfloat16)
    )
    gate = jax.nn.sigmoid(jnp.dot(embedded, gate_weight.T, preferred_element_type=jnp.float32))
    projected = jnp.einsum(
        "bn,enr->ebr",
        embedded,
        lax.all_gather(cross_in, "dp", axis=1, tiled=True),
        preferred_element_type=jnp.float32,
    )
    hidden = jnp.tanh(projected).astype(jnp.bfloat16)
    mixed = jnp.tanh(
        jnp.einsum("ebr,erq->ebq", hidden, cross_mix, preferred_element_type=jnp.float32)
    ).astype(jnp.bfloat16)
    gate_columns = gate.T
    grown = jnp.einsum(
        "ebr,ern->ebn",
        mixed,
        lax.all_gather(cross_out, "dp", axis=2, tiled=True),
        preferred_element_type=jnp.float32,
    )
    grown = grown + cross_bias[:, None, :]
    weighted = jnp.sum(gate_columns[:, :, None] * grown, axis=0)
    base = embedded.astype(jnp.float32)
    return (base + base * weighted).astype(jnp.bfloat16)


def solution(mesh):
    in_specs = (
        P(None, "mp", None),
        P(("mp", "dp"), None),
        P(("mp", "dp"), None),
        P(("mp", "dp")),
        P(("mp", "dp"), None),
        P(("mp", "dp")),
        P(("mp", "dp")),
        P(None, "dp", None),
        P(),
        P(None, None, "dp"),
        P(),
        P(),
    )
    out_specs = P(("mp", "dp"), None)
    return jax.shard_map(
        on_device, mesh=mesh, in_specs=in_specs, out_specs=out_specs, check_vma=False
    )
```

profile of v0, /device:TPU:8, one launch (start us, length us, event | category | flops | bytes accessed | tf_op | source)
XLA Modules:
  0.0 309.0 jit_solution(1499856670255202471)
XLA Ops:
  6.5 0.0 copy-start
  6.5 0.0 all-gather.3.cloned.1.call-start
  6.5 0.7 all-gather.3.cloned.1.call-update
  7.9 0.7 fusion.25
  8.7 0.1 reduce_window_sum.11
  8.8 0.8 select_reduce_fusion
  9.6 0.7 broadcast_multiply_fusion
  10.3 0.7 fusion.38
  10.9 1.6 scatter_custom_fusion
  12.6 11.3 %all-to-all-start = ((s32[32,4,128]{2,1,0:T(4,128)}), s32[32,4,128]{2,1,0:T(4,128)S(1)}, u32[]{:S(2)}, u32[]{:S(2)}) async-start(s32[32,4,128]{2,1,0:T(4,128)} %bitcast.7), calls=%async_computation | async-start | bytes 131072 | tf_op jit(solution)/shard_map/all_to_all | solution.py:76
  23.9 0.5 broadcast_in_dim.29
  24.4 58.5 %while.10 = (s32[]{:T(128)}, bf16[64,128,128]{2,1,0:T(8,128)(2,1)S(1)}, s32[]{:T(128)}, s32[64]{0:T(128)}, s32[64,128]{1,0:T(8,128)}, /*index=5*/bf16[20,2048,12...) while((s32[]{:T(128)}, bf16[64,128,128]{2,1,0:T(8,128)(2,1)S(1)}, s32[]{:T(128)}, ...), condition=%wide.region_6.7_spmd, body=%wide.region_5.6_spmd.sunk | while | flops 6190 | bytes 1065215 | solution.py:48
  24.4 0.7 fusion.52
  25.2 0.8 fusion.53
  25.9 12.9 %gather_fusion = bf16[1024,128]{1,0:T(8,128)(2,1)S(1)} fusion(bf16[20,2048,128]{2,1,0:T(8,128)(2,1)} %get-tuple-element.117, s32[1024]{0:T(1024)S(1)} %fusion.53), kind=kCustom, calls=%fused_computation.clone.1 | custom fusion | bytes 532480 | tf_op jit(solution)/shard_map/while/body/gather | solution.py:15
  38.9 0.7 fusion.52
  39.7 0.8 fusion.53
  40.4 12.9 %gather_fusion = bf16[1024,128]{1,0:T(8,128)(2,1)S(1)} fusion(bf16[20,2048,128]{2,1,0:T(8,128)(2,1)} %get-tuple-element.117, s32[1024]{0:T(1024)S(1)} %fusion.53), kind=kCustom, calls=%fused_computation.clone.1 | custom fusion | bytes 532480 | tf_op jit(solution)/shard_map/while/body/gather | solution.py:15
  53.4 0.7 fusion.52
  54.1 0.8 fusion.53
  54.8 13.2 %gather_fusion = bf16[1024,128]{1,0:T(8,128)(2,1)S(1)} fusion(bf16[20,2048,128]{2,1,0:T(8,128)(2,1)} %get-tuple-element.117, s32[1024]{0:T(1024)S(1)} %fusion.53), kind=kCustom, calls=%fused_computation.clone.1 | custom fusion | bytes 532480 | tf_op jit(solution)/shard_map/while/body/gather | solution.py:15
  68.1 0.7 fusion.52
  68.9 0.8 fusion.53
  69.6 13.2 %gather_fusion = bf16[1024,128]{1,0:T(8,128)(2,1)S(1)} fusion(bf16[20,2048,128]{2,1,0:T(8,128)(2,1)} %get-tuple-element.117, s32[1024]{0:T(1024)S(1)} %fusion.53), kind=kCustom, calls=%fused_computation.clone.1 | custom fusion | bytes 532480 | tf_op jit(solution)/shard_map/while/body/gather | solution.py:15
  82.9 3.0 broadcast_in_dim.28
  85.9 8.0 %scatter_fusion = bf16[128,128,128]{2,1,0:T(8,128)(2,1)} fusion(bf16[128,128,128]{2,1,0:T(8,128)(2,1)} %broadcast_in_dim.28, s32[64]{0:T(128)S(1)} %fusion.38, bf16[64,128,128]{2,1,0:T(8,128)(2,1)S(1)} %get-tuple-element.38), kind=kCustom, calls=%fused_computation.2 | custom fusion | bytes 6291712 | tf_op jit(solution)/shard_map/scatter | solution.py:63
  94.0 0.0 all-to-all-done
  94.0 64.9 %all-to-all-start.1 = ((bf16[32,4,128,128]{3,2,1,0:T(8,128)(2,1)}), bf16[32,4,128,128]{3,2,1,0:T(8,128)(2,1)}, u32[]{:S(2)}, u32[]{:S(2)}) async-start(bf16[32,4,128,128]{3,2,1,0:T(8,128)(2,1)} %bitcast.58), calls=%async_computation.1 | async-start | bytes 8388608 | tf_op jit(solution)/shard_map/all_to_all | solution.py:69
  158.9 0.2 all-gather.5.cloned.1.call-start
  159.1 0.5 all-gather.5.cloned.1.call-update
  159.6 0.6 reduce_max.9
  160.3 0.7 convert_reduce_fusion
  161.0 0.1 and.121
  161.1 0.1 and.113
  161.2 0.1 div.27
  161.4 94.6 %all-to-all-done.1 = bf16[32,4,128,128]{3,2,1,0:T(8,128)(2,1)} async-done(((bf16[32,4,128,128]{3,2,1,0:T(8,128)(2,1)}), bf16[32,4,128,128]{3,2,1,0:T(8,128)(2,1)}, u32[]{:S(2)}, u32[]{:S(2)}) %all-to-all-start.1) | async-done | bytes 4194336 | tf_op jit(solution)/shard_map/all_to_all | solution.py:69
  256.0 5.8 %fusion.7 = bf16[128,128,128]{2,1,0:T(8,128)(2,1)} fusion(bf16[128,128,128]{2,1,0:T(8,128)(2,1)} %bitcast.11, s32[128,128]{1,0:T(8,128)S(1)} %fusion.19), kind=kOutput, calls=%fused_computation.15 | convolution fusion | flops 538968064 | bytes 8454144 | tf_op jit(solution)/shard_map/kis,kiw->ksw/dot_general | solution.py:88
  261.8 7.1 %reshape.165 = bf16[32,4,16384]{2,1,0:T(4,128)(2,1)} reshape(bf16[128,128,128]{2,1,0:T(8,128)(2,1)} %fusion.7) | data formatting | bytes 8388608 | tf_op jit(solution)/shard_map/reshape | solution.py:100
  268.8 6.6 %convolution_convert_fusion = bf16[32,4,16384]{2,1,0:T(4,128)(2,1)} fusion(bf16[32,4,16384]{2,1,0:T(4,128)(2,1)} %reshape.165, s32[32,4]{1,0:T(8,128)S(1)} %get-tuple-element.51, pred[32,4]{1,0:T(8,128)(4,1)S(1)} %broadcast_compare_fusion), kind=kOutput, calls=%fused_computation.13 | convolution fusion | flops 16778752 | bytes 8389248 | tf_op jit(solution)/shard_map/pkj,pjx->pkx/dot_general | solution.py:99
  275.4 6.9 %reshape.166 = bf16[128,16384]{1,0:T(8,128)(2,1)} reshape(bf16[32,4,16384]{2,1,0:T(4,128)(2,1)} %convolution_convert_fusion) | data formatting | bytes 8388608 | tf_op jit(solution)/shard_map/reshape | solution.py:109
  282.3 6.4 %copy.17 = bf16[16384,128]{1,0:T(8,128)(2,1)} copy(bf16[16384,128]{0,1:T(8,128)(2,1)} %bitcast.61) | data formatting | bytes 8388608 | tf_op jit(solution)/shard_map/kt,kx->tx/dot_general | solution.py:109
  288.7 0.0 copy-start.1
  288.7 3.4 %fusion.10 = bf16[128,20,128]{2,1,0:T(8,128)(2,1)S(1)} fusion(bf16[128,128,128]{2,1,0:T(8,128)(2,1)} %bitcast.60, s32[128]{0:T(128)S(1)} %add_select_fusion.2, pred[128]{0:T(512)(128)(4,1)S(1)} %and.121), kind=kOutput, calls=%fused_computation.21 | convolution fusion | flops 84218880 | bytes 4850304 | tf_op jit(solution)/shard_map/kt,kx->tx/dot_general | solution.py:109
  292.1 0.5 copy.18
  292.6 0.0 copy-start.2
  292.6 0.2 copy.19
  292.8 0.0 copy-done.1
  292.8 0.2 fusion.17
  293.0 0.0 all-gather.3.cloned.1.call-done
  293.1 0.0 copy-done
  293.1 3.5 %fusion.12 = bf16[4,128,256]{2,1,0:T(8,128)(2,1)S(1)} fusion(bf16[4,256,256]{2,1,0:T(8,128)(2,1)S(1)} %copy-done, bf16[128,2560,1]{0,1,2:T(8,128)(2,1)S(1)} %bitcast.64, bf16[4,2560,256]{2,1,0:T(8,128)(2,1)} %all-gather.3.cloned.1.call-done), kind=kOutput, calls=%fused_computation.25 | convolution fusion | flops 738459648 | bytes 6684672 | tf_op jit(solution)/shard_map/ebr,erq->ebq/dot_general | solution.py:125
  296.6 0.0 all-gather.5.cloned.1.call-done
  296.7 0.0 copy-done.2
  296.7 4.5 %multiply_reduce_fusion = f32[128,2560]{1,0:T(8,128)S(1)} fusion(bf16[4,128,256]{2,1,0:T(8,128)(2,1)S(1)} %fusion.12, bf16[4,256,2560]{1,2,0:T(8,128)(2,1)} %all-gather.5.cloned.1.call-done, f32[4,2560]{1,0:T(4,128)S(1)} %copy-done.2, f32[4,128]{1,0:T(4,128)S(1)} %fusion.17), kind=kOutput, calls=%fused_computation.16 | convolution fusion | flops 674693120 | bytes 6858752 | tf_op jit(solution)/shard_map/ebr,ern->ebn/dot_general | solution.py:128
  301.2 1.0 fusion.9
  (11 shorter events, 0.2 us)
Async XLA Ops:
  6.5 286.5 %copy-start = (bf16[4,256,256]{2,1,0:T(8,128)(2,1)S(1)}, bf16[4,256,256]{2,1,0:T(8,128)(2,1)}, u32[]{:S(2)}) copy-start(bf16[4,256,256]{2,1,0:T(8,128)(2,1)} %param.22) | copy-start | bytes 1572868
  6.5 286.5 %all-gather.3.cloned.1.call-start = ((), (), s32[]{:S(2)}) async-start(), calls=%async_computation.2 | async-start | bytes 5898240 | tf_op jit(solution)/shard_map/all_gather | solution.py:120
  12.6 81.4 %all-to-all-start = ((s32[32,4,128]{2,1,0:T(4,128)}), s32[32,4,128]{2,1,0:T(4,128)S(1)}, u32[]{:S(2)}, u32[]{:S(2)}) async-start(s32[32,4,128]{2,1,0:T(4,128)} %bitcast.7), calls=%async_computation | async-start | bytes 131072 | tf_op jit(solution)/shard_map/all_to_all | solution.py:76
  94.0 162.0 %all-to-all-start.1 = ((bf16[32,4,128,128]{3,2,1,0:T(8,128)(2,1)}), bf16[32,4,128,128]{3,2,1,0:T(8,128)(2,1)}, u32[]{:S(2)}, u32[]{:S(2)}) async-start(bf16[32,4,128,128]{3,2,1,0:T(8,128)(2,1)} %bitcast.58), calls=%async_computation.1 | async-start | bytes 8388608 | tf_op jit(solution)/shard_map/all_to_all | solution.py:69
  158.9 137.8 %all-gather.5.cloned.1.call-start = ((), (), s32[]{:S(2)}) async-start(), calls=%async_computation.3 | async-start | bytes 5898240 | tf_op jit(solution)/shard_map/all_gather | solution.py:131
  288.7 4.2 %copy-start.1 = (bf16[4,2560]{1,0:T(4,128)(2,1)S(1)}, bf16[4,2560]{1,0:T(4,128)(2,1)}, u32[]{:S(2)}) copy-start(bf16[4,2560]{1,0:T(4,128)(2,1)} %param.25) | copy-start | bytes 61444
  292.6 4.1 %copy-start.2 = (f32[4,2560]{1,0:T(4,128)S(1)}, f32[4,2560]{1,0:T(4,128)}, u32[]{:S(2)}) copy-start(f32[4,2560]{1,0:T(4,128)} %param.24) | copy-start | bytes 122884
Sparse Core Ops, SparseCore 0:
  9.2 40.9 all-gather.2
  161.5 42.8 all-gather.4
where the time goes:
time: 314 us; the launch traced here: 309 us
  waiting for transfers between devices  95.8 us (31%)
  local copies, waits for them, and re-layouts  85.3 us (27%)
  starting transfers between devices  76.4 us (24%)
  matrix products  24 us (8%)
  between operations  14.3 us (5%)
  other arithmetic  13 us (4%)
    all_to_all x1, waiting for transfers between devices, on_device(): lax.all_to_all(send_rows.reshape(peers, capacity, block_width, width), 'm...  94.6 us
    all_to_all x1, starting transfers between devices, on_device(): lax.all_to_all(send_rows.reshape(peers, capacity, block_width, width), 'm...  64.9 us
    gather x4, local copies, waits for them, and re-layouts, pick_rows(): return tables[table_ids[:, None], row_ids]  52.1 us
    all_to_all x1, starting transfers between devices, on_device(): lax.all_to_all(send_code.reshape(peers, capacity, block_width), 'mp', spl...  11.3 us
    scatter x1, local copies, waits for them, and re-layouts, on_device(): send_rows = jnp.zeros((peers * capacity, block_width, width), jnp.bfloat1...  8.05 us
    reshape x1, local copies, waits for them, and re-layouts, on_device(): contrib.reshape(peers, capacity, samples * width)  7.05 us
    reshape x1, local copies, waits for them, and re-layouts, on_device(): rounded.reshape(peers * capacity, samples * width)  6.92 us
    dot_general x1, matrix products, on_device(): jnp.einsum('pkj,pjx->pkx', same.astype(jnp.float32), contrib.reshape(peer...  6.56 us
  transfers between devices with their start and end apart: 4, of which 1 were waited for; matrix products, arithmetic and copies ran while one was open for 38% of the time, Pallas kernels for 0%

commit v1 on v0

v1 whole, which is shorter than its diff:
```python
import jax
import jax.numpy as jnp
from jax import lax
from jax.experimental import pallas as pl
from jax.experimental.pallas import tpu as pltpu
from jax.sharding import PartitionSpec as P

UNIT = 16
LANES = 128


def block_meta(block_slots, block_table, block_peer, block_len, count, peers, tables):
    blocks, width = block_slots.shape
    ids = jnp.arange(blocks, dtype=jnp.int32)
    live = ids < count
    lens = jnp.where(live, block_len, 0)
    entry_live = jnp.arange(width, dtype=jnp.int32)[None, :] < lens[:, None]
    slots = jnp.where(entry_live, block_slots, -1)
    samples = jnp.arange(LANES, dtype=jnp.int32)
    hit = slots[:, :, None] == samples[None, None, :]
    present = jnp.any(hit, axis=1)
    upper = (samples[:, None] < samples[None, :]).astype(jnp.bfloat16)
    rank = jnp.dot(present.astype(jnp.bfloat16), upper, preferred_element_type=jnp.float32).astype(jnp.int32)
    rows = jnp.sum(present.astype(jnp.int32), axis=1)
    rank_slot = jnp.where(present, rank, -1)
    rank_entry = jnp.max(jnp.where(hit, rank[:, None, :], -1), axis=2)
    units = (rows + UNIT - 1) // UNIT
    same = (block_peer[:, None] == block_peer[None, :]) & live[None, :] & (ids[None, :] < ids[:, None])
    position = jnp.sum(same.astype(jnp.int32), axis=1)
    start = jnp.sum(jnp.where(same, units[None, :], 0), axis=1)
    total = jnp.max(jnp.where(live, start + units, 0))
    key = jnp.where(live, block_table, tables) * blocks + ids
    place = jnp.sum((key[None, :] < key[:, None]).astype(jnp.int32), axis=1)
    order = jnp.sum(jnp.where(place[None, :] == ids[:, None], ids[None, :], 0), axis=1)
    bounds = jnp.sum(
        (live[None, :] & (block_table[None, :] < jnp.arange(blocks, dtype=jnp.int32)[:, None])).astype(jnp.int32), axis=1
    )
    return dict(live=live, lens=lens, rank_slot=rank_slot, rank_entry=rank_entry, units=units, position=position,
                start=start, total=total, order=order, bounds=bounds)


def pack_kernel(meta, rows, rank, tables_hbm, out, stage, wide, picked, sems):
    tables, rows_dev, width = tables_hbm.shape

    def copy(t):
        return pltpu.make_async_copy(tables_hbm.at[t], stage.at[t], sems.at[t])

    for t in range(tables):
        copy(t).start()
    picked[...] = jnp.zeros_like(picked)

    def clear(p, carry):
        out[p] = jnp.zeros(out.shape[1:], out.dtype)
        return carry

    lax.fori_loop(0, out.shape[0], clear, 0)
    unit_rows = lax.broadcasted_iota(jnp.int32, (LANES, LANES), 0)

    def one_block(k, carry):
        b = meta[0, k]
        length = meta[1, b]
        units = meta[2, b]
        first = meta[3, b]
        peer = meta[4, b]

        def eight(i, c):
            base = pl.multiple_of(i * 8, 8)
            got = [wide[pl.ds(rows[b, base + j], 1), :] for j in range(8)]
            picked[pl.ds(base, 8), :] = jnp.concatenate(got, axis=0)
            return c

        lax.fori_loop(0, (length + 7) // 8, eight, 0)
        choose = (rank[pl.ds(b, 1), :] == unit_rows).astype(jnp.float32).astype(jnp.bfloat16)
        packed = jnp.dot(choose, picked[...].astype(jnp.bfloat16), preferred_element_type=jnp.float32)
        packed = packed.astype(jnp.bfloat16)
        for u in range(LANES // UNIT):
            @pl.when(u < units)
            def _():
                out[peer, pl.ds(pl.multiple_of((first + u) * UNIT, UNIT), UNIT), :] = packed[u * UNIT:(u + 1) * UNIT]
        return carry

    def one_table(t, carry):
        copy(t).wait()
        lo = meta[5, t]
        hi = meta[5, t + 1]

        @pl.when(hi > lo)
        def _():
            def widen(i, c):
                at = pl.multiple_of(i * 256, 256)
                wide[pl.ds(at, 256), :] = stage[t, pl.ds(at, 256), :].astype(jnp.float32)
                return c

            lax.fori_loop(0, rows_dev // 256, widen, 0)
            lax.fori_loop(lo, hi, one_block, 0)

        return carry

    lax.fori_loop(0, tables, one_table, 0)


def pack(meta, rows, rank, tables, peers, cap_rows):
    count, rows_dev, width = tables.shape
    return pl.pallas_call(
        pack_kernel,
        out_shape=jax.ShapeDtypeStruct((peers, cap_rows, width), jnp.bfloat16),
        in_specs=[
            pl.BlockSpec(memory_space=pltpu.SMEM),
            pl.BlockSpec(memory_space=pltpu.SMEM),
            pl.BlockSpec(memory_space=pltpu.VMEM),
            pl.BlockSpec(memory_space=pltpu.HBM),
        ],
        out_specs=pl.BlockSpec(memory_space=pltpu.VMEM),
        scratch_shapes=[
            pltpu.VMEM((count, rows_dev, width), jnp.bfloat16),
            pltpu.VMEM((rows_dev, width), jnp.float32),
            pltpu.VMEM((LANES, width), jnp.float32),
            pltpu.SemaphoreType.DMA((count,)),
        ],
        compiler_params=pltpu.CompilerParams(vmem_limit_bytes=40 * 2**20),
        name="pack_rows",
    )(meta, rows, rank, tables)


def unpack_kernel(meta, rank, rows, out):
    tables = out.shape[1] // LANES
    last = rows.shape[0] - LANES
    row_ids = lax.broadcasted_iota(jnp.int32, (LANES, LANES), 0)

    def one_table(t, carry):
        lo = meta[1, t]
        hi = meta[1, t + 1]

        def one_pair(i, acc):
            picks, parts = [], []
            for j in range(2):
                k = lo + 2 * i + j
                b = meta[0, jnp.minimum(k, hi - 1)]
                first = meta[2, b]
                base = jnp.minimum(first, last)
                skip = jnp.where(k < hi, first - base, 2 * LANES)
                picks.append(rank[pl.ds(b, 1), :] + skip == row_ids)
                parts.append(rows[pl.ds(pl.multiple_of(base, UNIT), LANES), :])
            choose = jnp.concatenate(picks, axis=0).astype(jnp.float32).astype(jnp.bfloat16)
            return acc + lax.dot_general(
                choose, jnp.concatenate(parts, axis=0), (((0,), (0,)), ((), ())), preferred_element_type=jnp.float32
            )

        total = lax.fori_loop(0, (hi - lo + 1) // 2, one_pair, jnp.zeros((LANES, LANES), jnp.float32))
        out[:, pl.ds(pl.multiple_of(t * LANES, LANES), LANES)] = total.astype(out.dtype)
        return carry

    lax.fori_loop(0, tables, one_table, 0)


def unpack(meta, rank, rows, tables):
    return pl.pallas_call(
        unpack_kernel,
        out_shape=jax.ShapeDtypeStruct((LANES, tables * LANES), jnp.bfloat16),
        in_specs=[
            pl.BlockSpec(memory_space=pltpu.SMEM),
            pl.BlockSpec(memory_space=pltpu.VMEM),
            pl.BlockSpec(memory_space=pltpu.VMEM),
        ],
        out_specs=pl.BlockSpec(memory_space=pltpu.VMEM),
        compiler_params=pltpu.CompilerParams(vmem_limit_bytes=40 * 2**20),
        name="unpack_rows",
    )(meta, rank, rows)


def make_header(m, block_table, block_peer, peers):
    blocks, width = m["rank_slot"].shape
    extra = jnp.stack([m["live"].astype(jnp.int32), block_table, m["start"]], axis=1)
    values = jnp.concatenate(
        [m["rank_slot"] + 1, extra, jnp.zeros((blocks, width - 3), jnp.int32)], axis=1
    ).astype(jnp.bfloat16)
    target = jnp.where(m["live"], block_peer * 4 + m["position"], -1)
    place = (target[None, :] == jnp.arange(4 * peers, dtype=jnp.int32)[:, None]).astype(jnp.bfloat16)
    spread = jnp.dot(place, values, preferred_element_type=jnp.float32).astype(jnp.bfloat16)
    return spread.reshape(peers, 4, 2 * width)


def read_header(header, tables):
    peers, each, wide = header.shape
    flat = header.reshape(peers * each, wide).astype(jnp.int32)
    rank = flat[:, :LANES] - 1
    live = flat[:, LANES] > 0
    table = jnp.where(live, flat[:, LANES + 1], tables)
    start = flat[:, LANES + 2]
    ids = jnp.arange(peers * each, dtype=jnp.int32)
    key = table * (peers * each) + ids
    place = jnp.sum((key[None, :] < key[:, None]).astype(jnp.int32), axis=1)
    order = jnp.sum(jnp.where(place[None, :] == ids[:, None], ids[None, :], 0), axis=1)
    bounds = jnp.sum((table[None, :] < ids[:, None]).astype(jnp.int32), axis=1)
    return rank, order, bounds, start


CAPS = (8, 12, 16, 18, 20, 22, 24, 28, 32)


def on_device(
    tables,
    block_rows,
    block_slots,
    block_table,
    block_peer,
    block_len,
    block_count,
    cross_in,
    cross_mix,
    cross_out,
    cross_bias,
    gate_weight,
):
    peers = lax.axis_size("mp")
    table_count = tables.shape[0]
    down = lax.all_gather(cross_in, "dp", axis=1, tiled=True)
    up = lax.all_gather(jnp.swapaxes(cross_out, 1, 2), "dp", axis=1, tiled=True)
    peer = block_peer[:, 0]
    m = block_meta(block_slots, block_table, peer, block_len, block_count[0], peers, table_count)
    header = lax.all_to_all(make_header(m, block_table, peer, peers), "mp", split_axis=0, concat_axis=0, tiled=True)
    most = lax.pmax(m["total"], ("mp", "dp"))
    table = jnp.stack([m["order"], m["lens"], m["units"], m["start"], peer, m["bounds"]])
    packed = pack(table, block_rows, m["rank_entry"], tables, peers, 4 * LANES)
    rank, order, bounds, start = read_header(header, table_count)

    def exchange(cap):
        def run(packed, rank, order, bounds, start):
            rows = cap * UNIT
            got = lax.all_to_all(packed[:, :rows], "mp", split_axis=0, concat_axis=0, tiled=True)
            source = jnp.arange(start.shape[0], dtype=jnp.int32) // 4
            meta = jnp.stack([order, bounds, source * rows + start * UNIT])
            return unpack(meta, rank, got.reshape(peers * rows, LANES), table_count)

        return run

    level = sum((most > cap).astype(jnp.int32) for cap in CAPS[:-1])
    embedded = lax.switch(level, [exchange(cap) for cap in CAPS], packed, rank, order, bounds, start)

    gate = jax.nn.sigmoid(jnp.dot(embedded, gate_weight.T, preferred_element_type=jnp.float32))
    projected = jnp.einsum("bn,enr->ebr", embedded, down, preferred_element_type=jnp.float32)
    hidden = jnp.tanh(projected).astype(jnp.bfloat16)
    mixed = jnp.tanh(
        jnp.einsum("ebr,erq->ebq", hidden, cross_mix, preferred_element_type=jnp.float32)
    ).astype(jnp.bfloat16)
    grown = jnp.einsum("ebr,enr->ebn", mixed, up, preferred_element_type=jnp.float32)
    grown = grown + cross_bias[:, None, :]
    weighted = jnp.sum(gate.T[:, :, None] * grown, axis=0)
    base = embedded.astype(jnp.float32)
    return (base + base * weighted).astype(jnp.bfloat16)


def solution(mesh):
    in_specs = (
        P(None, "mp", None),
        P(("mp", "dp"), None),
        P(("mp", "dp"), None),
        P(("mp", "dp")),
        P(("mp", "dp"), None),
        P(("mp", "dp")),
        P(("mp", "dp")),
        P(None, "dp", None),
        P(),
        P(None, None, "dp"),
        P(),
        P(),
    )
    return jax.shard_map(
        on_device, mesh=mesh, in_specs=in_specs, out_specs=P(("mp", "dp"), None), check_vma=False
    )
```

time: 314 us -> 244 us (0.78)
  the two profiles are of different devices: /device:TPU:8 before, /device:TPU:30 now
where the time goes in v1:
time: 244 us; the launch traced here: 239 us
  blocking collectives  74.9 us (31%)
  waiting for transfers between devices  61.3 us (25%)
  starting transfers between devices  35.5 us (15%)
  between operations  19.6 us (8%)
  Pallas kernels  15.6 us (6%)
  other arithmetic  11.3 us (5%)
  local copies, waits for them, and re-layouts  11.1 us (5%)
  matrix products  9.82 us (4%)
    pmax x1, blocking collectives, on_device(): most = lax.pmax(m['total'], ('mp', 'dp'))  74.9 us
    all_to_all x1, waiting for transfers between devices, run(): lax.all_to_all(packed[:, :rows], 'mp', split_axis=0, concat_axis=0, tiled...  59.9 us
    all_to_all x1, starting transfers between devices, run(): lax.all_to_all(packed[:, :rows], 'mp', split_axis=0, concat_axis=0, tiled...  23.9 us
    all_to_all x1, starting transfers between devices, on_device(): lax.all_to_all(make_header(m, block_table, peer, peers), 'mp', split_axis...  11.6 us
    pallas_call x1, Pallas kernels, pack(): pl.pallas_call(pack_kernel, out_shape=jax.ShapeDtypeStruct((peers, cap_ro...  9.88 us
    unnamed x9, local copies, waits for them, and re-layouts  5.85 us
    pallas_call x1, Pallas kernels, unpack(): pl.pallas_call(unpack_kernel, out_shape=jax.ShapeDtypeStruct((LANES, tabl...  5.75 us
  transfers between devices with their start and end apart: 4, of which 1 were waited for; matrix products, arithmetic and copies ran while one was open for 9% of the time, Pallas kernels for 7%

profile of v1, /device:TPU:30, one launch (start us, length us, event | category | flops | bytes accessed | tf_op | source)
XLA Modules:
  0.0 239.2 jit_solution(14384337691208805427)
XLA Ops:
  6.5 0.0 copy-start
  6.5 0.0 all-gather.3.cloned.1.call-start
  6.5 0.7 all-gather.3.cloned.1.call-update
  7.3 0.0 all-gather.5.cloned.1.call-start
  7.3 0.7 all-gather.5.cloned.1.call-update
  8.7 0.7 broadcast_select_fusion
  9.3 0.8 fusion.32
  10.2 1.4 fusion.18
  11.6 0.1 add_convert_fusion
  11.7 1.0 convert_reduce_fusion.2
  12.7 1.4 iota_add_fusion
  14.0 0.1 copy.20
  14.2 0.1 copy.21
  14.3 0.1 copy.19
  14.4 0.1 concatenate.4
  14.5 0.7 add_select_fusion
  15.2 0.1 convolution_convert_fusion
  15.3 0.7 reshape.473
  16.0 11.6 %all-to-all-start.9 = ((bf16[32,4,256]{2,1,0:T(4,128)(2,1)}), bf16[32,4,256]{2,1,0:T(4,128)(2,1)S(1)}, u32[]{:S(2)}, u32[]{:S(2)}) async-start(bf16[32,4,256]{2,1,0:T(4,128)(2,1)} %reshape.473), calls=%async_computation.9 | async-start | bytes 131072 | tf_op jit(solution)/shard_map/all_to_all | solution.py:221
  27.6 74.9 %pmax.7 = s32[]{:T(128)} all-reduce(s32[]{:T(128)} %get-tuple-element.376), channel_id=1, replica_groups=mesh['mp'=32,'dp'=8] {'mp','dp'}, use_global_device_ids=true, to_apply=%region_4.5 | all-reduce | flops 1 | bytes 8 | tf_op jit(solution)/shard_map/pmax | solution.py:222
  107.8 0.2 convert_reduce_fusion.1
  108.0 0.1 select_reduce_fusion.10
  108.1 0.7 fusion.44
  108.8 0.7 stack.121.meta
  109.5 2.6 %select_reduce_fusion.9.rank = s32[64,128]{1,0:T(8,128)S(1)} fusion(s32[64,128]{1,0:T(8,128)S(1)} %get-tuple-element.375, s32[64,128]{1,0:T(8,128)S(1)} %fusion.32), kind=kLoop, calls=%fused_computation.91 | loop fusion | flops 3137536 | bytes 98304 | tf_op jit(solution)/shard_map/reduce_max | solution.py:26
  112.1 0.0 copy-start.1
  112.1 4.0 %copy-done.1 = bf16[20,2048,128]{2,1,0:T(8,128)(2,1)S(1)} copy-done((bf16[20,2048,128]{2,1,0:T(8,128)(2,1)S(1)}, bf16[20,2048,128]{2,1,0:T(8,128)(2,1)}, u32[]{:S(2)}) %copy-start.1) | copy-done | bytes 10485784
  116.0 0.0 copy-start.2
  116.0 0.8 copy-done.2
  116.8 9.9 %pack_rows.1 = bf16[32,512,128]{2,1,0:T(8,128)(2,1)} custom-call(s32[6,64]{1,0:T(8,128)S(1)} %stack.121.meta, s32[64,128]{1,0:T(8,128)S(1)} %copy-done.2, s32[64,128]{1,0:T(8,128)S(1)} %select_reduce_fusion.9.rank, bf16[20,2048,128]{2,1,0:T(8,128)(2,1)S(1)} %copy-done.1), custom_call_target="tpu_custom_call" | custom-call | tf_op jit(solution)/shard_map/pack_rows/pallas_call | solution.py:104
  126.7 0.0 all-to-all-done.9
  126.8 0.2 add_reduce_fusion
  127.0 0.1 compare_convert_fusion
  127.1 94.6 %conditional.4 = (bf16[128,2560]{1,0:T(8,128)(2,1)}, bf16[128,2560]{1,0:T(8,128)(2,1)S(1)}) conditional(s32[]{:T(128)} %clamp.3, (s32[128,128]{1,0:T(8,128)S(1)}, s32[128,128]{1,0:T(8,128)S(1)}, s32[128,128]{1,0:T(8,128)S(1)}, s32[128,128]{1,0:T(8,128)S(1)}, s32[128,256]{1,0:T(8,128)S(1)}, ...), branch_computations={%region_10.14_spmd, %region_14.18_spmd, %region_18.22_spmd, %regio... | conditional | flops 100096 | bytes 20061240
  127.1 3.4 %slice.72 = bf16[32,320,128]{2,1,0:T(8,128)(2,1)} slice(bf16[32,512,128]{2,1,0:T(8,128)(2,1)} %get-tuple-element.313), slice={[0:32], [0:320], [0:128]} | slice | bytes 5242880 | tf_op jit(solution)/shard_map/cond/branch_4_fun/slice | solution.py:230
  130.5 23.9 %all-to-all-start.4 = ((bf16[32,320,128]{2,1,0:T(8,128)(2,1)}), bf16[32,320,128]{2,1,0:T(8,128)(2,1)S(1)}, u32[]{:S(2)}, u32[]{:S(2)}) async-start(bf16[32,320,128]{2,1,0:T(8,128)(2,1)} %slice.72), calls=%async_computation.4 | async-start | bytes 5242880 | tf_op jit(solution)/shard_map/cond/branch_4_fun/all_to_all | solution.py:230
  154.4 0.1 reduce_sum.151
  154.5 0.1 reduce_sum.153
  154.7 0.2 multiply_reduce_fusion.4
  154.9 0.1 slice_add_fusion.4
  155.0 59.9 %all-to-all-done.4 = bf16[32,320,128]{2,1,0:T(8,128)(2,1)S(1)} async-done(((bf16[32,320,128]{2,1,0:T(8,128)(2,1)}), bf16[32,320,128]{2,1,0:T(8,128)(2,1)S(1)}, u32[]{:S(2)}, u32[]{:S(2)}) %all-to-all-start.4) | async-done | bytes 2621472 | tf_op jit(solution)/shard_map/cond/branch_4_fun/all_to_all | solution.py:230
  214.9 5.8 %unpack_rows.13 = bf16[128,2560]{1,0:T(8,128)(2,1)} custom-call(s32[3,128]{1,0:T(4,128)S(1)} %pad_add_fusion.4.meta, s32[128,128]{1,0:T(8,128)S(1)} %get-tuple-element.359.rank, bf16[10240,128]{1,0:T(8,128)(2,1)S(1)} %bitcast.92), custom_call_target="tpu_custom_call" | custom-call | tf_op jit(solution)/shard_map/cond/branch_4_fun/unpack_rows/pallas_call | solution.py:157
  220.6 1.1 copy.31
  221.7 0.0 copy-start.8
  221.7 1.4 fusion.26
  223.1 0.0 all-gather.3.cloned.1.call-done
  223.1 0.0 copy-done
  223.1 3.7 %fusion.21 = bf16[4,128,256]{2,1,0:T(8,128)(2,1)S(1)} fusion(bf16[4,256,256]{2,1,0:T(8,128)(2,1)S(1)} %copy-done, bf16[4,2560,256]{2,1,0:T(8,128)(2,1)} %all-gather.3.cloned.1.call-done, bf16[128,2560]{1,0:T(8,128)(2,1)} %get-tuple-element.341), kind=kOutput, calls=%fused_computation.99 | convolution fusion | flops 738459648 | bytes 6684672 | tf_op jit(solution)/shard_map/ebr,erq->ebq/dot_general | solution.py:244
  226.8 0.0 all-gather.5.cloned.1.call-done
  226.8 0.0 copy-done.8
  226.9 4.5 %multiply_reduce_fusion.9 = f32[128,2560]{1,0:T(8,128)S(1)} fusion(bf16[4,128,256]{2,1,0:T(8,128)(2,1)S(1)} %fusion.21, bf16[4,2560,256]{2,1,0:T(8,128)(2,1)} %all-gather.5.cloned.1.call-done, f32[4,2560]{1,0:T(4,128)S(1)} %copy-done.8, f32[4,128]{1,0:T(4,128)S(1)} %fusion.26), kind=kOutput, calls=%fused_computation.90 | convolution fusion | flops 674693120 | bytes 6858752 | tf_op jit(solution)/shard_map/ebr,enr->ebn/dot_general | solution.py:246
  231.3 1.0 fusion.19
  (13 shorter events, 0.2 us)
Async XLA Ops:
  6.5 216.6 %copy-start = (bf16[4,256,256]{2,1,0:T(8,128)(2,1)S(1)}, bf16[4,256,256]{2,1,0:T(8,128)(2,1)}, u32[]{:S(2)}) copy-start(bf16[4,256,256]{2,1,0:T(8,128)(2,1)} %param.29) | copy-start | bytes 1572868
  6.5 216.5 %all-gather.3.cloned.1.call-start = ((), (), s32[]{:S(2)}) async-start(), calls=%async_computation.10 | async-start | bytes 5898240 | tf_op jit(solution)/shard_map/all_gather | solution.py:217
  7.3 219.6 %all-gather.5.cloned.1.call-start = ((), (), s32[]{:S(2)}) async-start(), calls=%async_computation.11 | async-start | bytes 5898240 | tf_op jit(solution)/shard_map/all_gather | solution.py:218
  16.0 110.7 %all-to-all-start.9 = ((bf16[32,4,256]{2,1,0:T(4,128)(2,1)}), bf16[32,4,256]{2,1,0:T(4,128)(2,1)S(1)}, u32[]{:S(2)}, u32[]{:S(2)}) async-start(bf16[32,4,256]{2,1,0:T(4,128)(2,1)} %reshape.473), calls=%async_computation.9 | async-start | bytes 131072 | tf_op jit(solution)/shard_map/all_to_all | solution.py:221
  112.1 4.0 %copy-start.1 = (bf16[20,2048,128]{2,1,0:T(8,128)(2,1)S(1)}, bf16[20,2048,128]{2,1,0:T(8,128)(2,1)}, u32[]{:S(2)}) copy-start(bf16[20,2048,128]{2,1,0:T(8,128)(2,1)} %tables_hbm.1) | copy-start | bytes 31457284
  116.0 0.8 copy-start.2
  130.5 84.3 %all-to-all-start.4 = ((bf16[32,320,128]{2,1,0:T(8,128)(2,1)}), bf16[32,320,128]{2,1,0:T(8,128)(2,1)S(1)}, u32[]{:S(2)}, u32[]{:S(2)}) async-start(bf16[32,320,128]{2,1,0:T(8,128)(2,1)} %slice.72), calls=%async_computation.4 | async-start | bytes 5242880 | tf_op jit(solution)/shard_map/cond/branch_4_fun/all_to_all | solution.py:230
  221.7 5.1 %copy-start.8 = (f32[4,2560]{1,0:T(4,128)S(1)}, f32[4,2560]{1,0:T(4,128)}, u32[]{:S(2)}) copy-start(f32[4,2560]{1,0:T(4,128)} %param.31) | copy-start | bytes 122884
Sparse Core Ops, SparseCore 0:
  9.2 40.4 all-gather.2
  51.5 39.0 all-gather.4
